TPU v7x, 256 devices: a whole 4x4x8 slice. The times are simulated.
256 devices in a mesh: group: 8 (over y, core), shard: 32 (over x, z).
Axes of the slice: x: 4, y: 4, z: 8, core: 2. Of those that a mesh axis runs over, the one named last changes fastest.
Arguments:
- params: float32 [4096, 7168], P(('group', 'shard')), may hold values from -3 to 3
- gradient: bfloat16 [4096, 7168], P(('group', 'shard'))
- first_moment: float32 [4096, 7168], P(('group', 'shard')), may hold values from -2 to 2
- second_moment: float32 [4096, 7168], P(('group', 'shard')), may hold values from 0.01 to 1
Outputs:
- new_params: float32 [4096, 7168], P(('group', 'shard'))
- new_first: float32 [4096, 7168], P(('group', 'shard'))
- new_second: float32 [4096, 7168], P(('group', 'shard'))
- replica: bfloat16 [4096, 7168], P('group')
All inputs are finite; a program needn't handle non-finite values.
Results may differ from a plain program's by a relative error of at most 0.00055.
Values may be sent and summed in bfloat16 or wider, within the bound.
A program may use at most 64 MiB of HBM per device.

v0:
```python
import jax
import jax.numpy as jnp
from jax import lax
from jax.sharding import PartitionSpec as P


def copy_for_each(x, axis):
    copies = jnp.broadcast_to(x, (lax.axis_size(axis), *x.shape))
    return lax.all_to_all(copies, axis, split_axis=0, concat_axis=0, tiled=True)


def taken_together(x, axis):
    return copy_for_each(x, axis).sum(axis=0)


def advance_rows(params, gradient, first_moment, second_moment, clip_scale):
    clipped = clip_scale * gradient.astype(jnp.float32)
    new_first = 0.9 * first_moment + 0.1 * clipped
    new_second = 0.95 * second_moment + 0.05 * clipped * clipped
    correct_one = 1.0 - 0.9**10
    correct_two = 1.0 - 0.95**10
    stepped = new_first / correct_one / (jnp.sqrt(new_second / correct_two) + 1e-08)
    new_params = params - 0.1 * (stepped + 0.1 * params)
    return (new_params, new_first, new_second, new_params.astype(jnp.bfloat16))


def on_device(params, gradient, first_moment, second_moment):
    grad_local = gradient.astype(jnp.float32)
    local_sum = jnp.sum(grad_local * grad_local)
    inner_sum = taken_together(local_sum, "shard")
    norm_total = taken_together(inner_sum, "group")
    entries = (
        gradient.shape[0] * gradient.shape[1] * lax.axis_size("group") * lax.axis_size("shard")
    )
    clip_scale = jnp.minimum(jnp.float32(1.0), 1.0 / jnp.sqrt(norm_total / entries + 1e-06))
    new_params, new_first, new_second, rounded = advance_rows(
        params, gradient, first_moment, second_moment, clip_scale
    )
    replica = lax.all_gather(rounded, "shard", axis=0, tiled=True)
    return (new_params, new_first, new_second, replica)


def solution(mesh):
    return jax.shard_map(
        on_device,
        mesh=mesh,
        in_specs=(
            P(("group", "shard"), None),
            P(("group", "shard"), None),
            P(("group", "shard"), None),
            P(("group", "shard"), None),
        ),
        out_specs=(
            P(("group", "shard"), None),
            P(("group", "shard"), None),
            P(("group", "shard"), None),
            P("group", None),
        ),
        check_vma=False,
    )
```

profile of v0, /device:TPU:8, one launch (start us, length us, event | category | flops | bytes accessed | tf_op | source)
XLA Modules:
  0.0 144.4 jit_solution(15113588647084784725)
XLA Ops:
  7.2 0.0 all-gather.2.cloned.1.call-start
  7.2 1.7 %fusion.2 = f32[]{:T(128)} fusion(bf16[16,7168]{1,0:T(8,128)(2,1)} %param.5), kind=kLoop, calls=%fused_computation.5 | loop fusion | flops 344063 | bytes 229380 | tf_op jit(solution)/shard_map/reduce_sum | solution.py:29
  8.9 0.7 broadcast_in_dim.6
  9.5 20.9 %all_to_all.12 = f32[32,1,1]{2,1,0:T(1,128)S(1)} all-to-all(f32[32,1,1]{2,1,0:T(1,128)S(1)} %broadcast_in_dim.6), channel_id=1, replica_groups=mesh['group'=8,'shard'=32] {'shard'}, dimensions={0} | all-to-all | bytes 256 | tf_op jit(solution)/shard_map/all_to_all | solution.py:9
  30.5 0.6 reduce_sum.28
  31.1 0.6 broadcast_in_dim.7
  31.8 8.5 %all_to_all.13 = f32[8,1,1]{2,1,0:T(1,128)S(1)} all-to-all(f32[8,1,1]{2,1,0:T(1,128)S(1)} %broadcast_in_dim.7), channel_id=1, replica_groups=mesh['group'=8,'shard'=32] {'group'}, dimensions={0} | all-to-all | bytes 64 | tf_op jit(solution)/shard_map/all_to_all | solution.py:9
  40.3 0.6 reduce_sum.29
  41.6 2.8 %fusion.4 = (bf16[16,7168]{1,0:T(8,128)(2,1)}, f32[16,7168]{1,0:T(8,128)}, f32[16,7168]{1,0:T(8,128)}, f32[16,7168]{1,0:T(8,128)}) fusion(f32[16,7168]{1,0:T(8,128)} %param.4, bf16[16,7168]{1,0:T(8,128)(2,1)} %param.5, f32[]{:T(128)S(6)} %min.3, f32[16,7168]{1,0:T(8,128)} %param.6, f32[16,7168]{1,0:T(8,128)} %param.7), kind=kLoop, calls=%fused_computation.8 | loop fusion | flops 2064384 | bytes 3211268 | tf_op jit(solution)/shard_map/convert_element_type | solution.py:24
  44.4 0.0 all-gather.2.cloned.1.call-update
  44.4 86.6 %all-gather.2.cloned.1.call-done = bf16[512,7168]{1,0:T(8,128)(2,1)} async-done(((bf16[16,7168]{1,0:T(8,128)(2,1)}), bf16[512,7168]{1,0:T(8,128)(2,1)}) %all-gather.2.cloned.1.call-update) | async-done | bytes 7340048 | tf_op jit(solution)/shard_map/all_gather | solution.py:39
  131.0 6.6 %copy.13 = bf16[512,7168]{1,0:T(8,128)(2,1)} copy(bf16[512,7168]{1,0:T(8,128)(2,1)} %all-gather.2.cloned.1.call-done) | data formatting | bytes 14680064
Async XLA Ops:
  7.2 123.8 %all-gather.2.cloned.1.call-start = ((), (), s32[]{:S(2)}) async-start(), calls=%async_computation.2 | async-start | bytes 7569408 | tf_op jit(solution)/shard_map/all_gather | solution.py:39
Sparse Core Ops, SparseCore 0:
  44.6 86.3 all-gather.1
where the time goes:
time: 145 us; the launch traced here: 144 us
  waiting for transfers between devices  86.6 us (60%)
  blocking collectives  29.5 us (20%)
  between operations  14.7 us (10%)
  local copies, waits for them, and re-layouts  7.9 us (5%)
  other arithmetic  5.71 us (4%)
    all_gather x1, waiting for transfers between devices, on_device(): replica = lax.all_gather(rounded, 'shard', axis=0, tiled=True)  86.6 us
    all_to_all x2, blocking collectives, copy_for_each(): return lax.all_to_all(copies, axis, split_axis=0, concat_axis=0, tiled=True)  29.5 us
    unnamed x1, local copies, waits for them, and re-layouts  6.6 us
  transfers between devices with their start and end apart: 1, of which 1 were waited for; matrix products, arithmetic and copies ran while one was open for 0% of the time, Pallas kernels for 0%

commit v1 on v0

v1 whole, which is shorter than its diff:
```python
import functools
import heapq
import itertools

import jax
import jax.numpy as jnp
from jax import lax
from jax.experimental import pallas as pl
from jax.experimental.pallas import tpu as pltpu
from jax.sharding import PartitionSpec as P

MESH = pl.DeviceIdType.MESH
NG, NX, NZ = 8, 4, 8
LANES = 128
ROWS = 8


def pieces_of(width):
    cut = (width // LANES * 23 // 56) * LANES
    return (
        (0, cut, width - cut, False, 1, 1),
        (8, cut, width - cut, False, -1, -1),
        (0, 0, cut, True, 1, 1),
        (8, 0, cut, True, -1, -1),
    )


def trees_of(pieces):
    sends = {}
    for v, (_, _, _, x_first, sx, sz) in enumerate(pieces):
        reach = {
            "x": {sx: NX // 2, -sx: NX // 2 - 1},
            "z": {sz: NZ // 2, -sz: NZ // 2 - 1},
        }
        first, second = ("x", "z") if x_first else ("z", "x")

        def add(axis, step, a, b, a2, b2):
            here = (a, b) if x_first else (b, a)
            there = (a2, b2) if x_first else (b2, a2)
            sends.setdefault((v, *here), []).append((axis, step, (v, *there)))

        for a in range(-reach[first][-1], reach[first][1] + 1):
            for step in (1, -1):
                if a * step >= 0 and abs(a) < reach[first][step]:
                    add(first, step, a, 0, a + step, 0)
            for step in (1, -1):
                for b in range(reach[second][step]):
                    add(second, step, a, b * step, a, (b + 1) * step)
    return sends


def order_of(pieces, sends, rate=46.6e3, latency=1.5):
    queues = {link: [] for link in itertools.product("xz", (1, -1))}
    free = dict.fromkeys(queues, 0.0)
    count = itertools.count()
    events = [(0.02 * v, next(count), (v, 0, 0)) for v in range(len(pieces))]
    events += [(0.0, next(count), None)]
    heapq.heapify(events)
    order = []
    while events:
        now, _, place = heapq.heappop(events)
        if place is not None:
            order.append(place)
            for axis, step, there in sends.get(place, ()):
                queues[axis, step].append(there)
        for link, queue in queues.items():
            if queue and free[link] <= now + 1e-9:
                there = queue.pop(0)
                free[link] = now + pieces[there[0]][2] * ROWS * 2 / rate
                heapq.heappush(events, (free[link], next(count), None))
                heapq.heappush(events, (free[link] + latency, next(count), there))
    return [place for place in order if place[1:] != (0, 0)]


def step_kernel(
    entries,
    p_hbm,
    g_hbm,
    m_hbm,
    v_hbm,
    rep,
    p_out,
    m_out,
    v_out,
    p_in,
    g_in,
    m_in,
    v_in,
    y_buf,
    x_buf,
    z_buf,
    load_sem,
    sum_send,
    sum_recv,
    send_sem,
    recv_sem,
):
    width = g_hbm.shape[1]
    group = lax.axis_index("group")
    shard = lax.axis_index("shard")
    x, z = shard // NZ, shard % NZ

    def at_group(k):
        return ((group + k) % NG, shard)

    def at(dx, dz):
        return (group, (x + dx + NX) % NX * NZ + (z + dz + NZ) % NZ)

    loads = [
        pltpu.make_async_copy(src, dst, load_sem.at[i])
        for i, (src, dst) in enumerate(
            ((g_hbm, g_in), (p_hbm, p_in), (m_hbm, m_in), (v_hbm, v_in))
        )
    ]
    for load in loads:
        load.start()

    stages = (
        (y_buf, [at_group(k) for k in range(1, NG)]),
        (x_buf, [at(k, 0) for k in range(1, NX)]),
        (z_buf, [at(0, k) for k in range(1, NZ)]),
    )
    barrier = pltpu.get_barrier_semaphore()
    peers = [peer for _, those in stages for peer in those]
    for peer in peers:
        pl.semaphore_signal(barrier, inc=1, device_id=peer, device_id_type=MESH)

    loads[0].wait()
    total = jnp.zeros((16, LANES), jnp.float32)
    for c in range(0, width, LANES):
        part = g_in[:, c : c + LANES].astype(jnp.float32)
        total = total + part * part
    total = jnp.sum(total, axis=0, keepdims=True)

    pl.semaphore_wait(barrier, len(peers))
    sent = []
    base = 0
    for buf, those in stages:
        buf[0] = total
        copies = [
            pltpu.make_async_remote_copy(
                src_ref=buf.at[0],
                dst_ref=buf.at[k],
                send_sem=sum_send.at[base + k - 1],
                recv_sem=sum_recv.at[base + k - 1],
                device_id=peer,
                device_id_type=MESH,
            )
            for k, peer in enumerate(those, 1)
        ]
        for copy in copies:
            copy.start()
        for copy in copies:
            copy.wait_recv()
        total = buf[0]
        for k in range(1, len(those) + 1):
            total = total + buf[k]
        sent += copies
        base += len(those)

    norm_total = jnp.sum(total, axis=1, keepdims=True)
    scale = jnp.minimum(1.0, 1.0 / jnp.sqrt(norm_total / entries + 1e-06))
    for load in loads[1:]:
        load.wait()

    pieces = pieces_of(width)
    sends = trees_of(pieces)
    order = order_of(pieces, sends)
    slot = {place: i for i, place in enumerate(order)}

    def view(place):
        v, ox, oz = place
        row, column, columns, *_ = pieces[v]
        source = (x - ox + NX) % NX * NZ + (z - oz + NZ) % NZ
        start = pl.multiple_of(source * 16 + row, 8)
        return rep.at[pl.ds(start, ROWS), pl.ds(column, columns)]

    def copy_to(axis, step, there):
        v, ox, oz = there
        here = (v, ox - step, oz) if axis == "x" else (v, ox, oz - step)
        return pltpu.make_async_remote_copy(
            src_ref=view(here),
            dst_ref=view(here),
            send_sem=send_sem.at[slot[there]],
            recv_sem=recv_sem.at[slot[there]],
            device_id=at(step, 0) if axis == "x" else at(0, step),
            device_id_type=MESH,
        )

    def forward(place):
        for axis, step, there in sends.get(place, ()):
            copy = copy_to(axis, step, there)
            copy.start()
            sent.append(copy)

    correct_one = 1.0 - 0.9**10
    correct_two = 1.0 - 0.95**10
    mine = pl.multiple_of(shard * 16, 16)
    chunk = 8 * LANES
    for v, (row, column, columns, *_) in enumerate(pieces):
        rows = slice(row, row + ROWS)
        for c in range(column, column + columns, chunk):
            cols = slice(c, min(c + chunk, column + columns))
            clipped = scale * g_in[rows, cols].astype(jnp.float32)
            params = p_in[rows, cols]
            new_first = 0.9 * m_in[rows, cols] + 0.1 * clipped
            new_second = 0.95 * v_in[rows, cols] + 0.05 * clipped * clipped
            stepped = (new_first / correct_one) / (
                jnp.sqrt(new_second / correct_two) + 1e-08
            )
            new_params = params - 0.1 * (stepped + 0.1 * params)
            p_out[rows, cols] = new_params
            m_out[rows, cols] = new_first
            v_out[rows, cols] = new_second
            rep[pl.ds(mine + row, ROWS), cols] = new_params.astype(jnp.bfloat16)
        forward((v, 0, 0))

    arrival = {
        there: (axis, step) for those in sends.values() for axis, step, there in those
    }
    for place in order:
        copy_to(*arrival[place], place).wait_recv()
        forward(place)
    for copy in sent:
        copy.wait_send()


def store_kernel(rep, p_new, m_new, v_new, p_out, m_out, v_out, rep_out, sem):
    parts = 8
    rows = rep.shape[0] // parts
    copies = [
        (rep.at[pl.ds(i * rows, rows)], rep_out.at[pl.ds(i * rows, rows)])
        for i in range(parts)
    ]
    copies += [(p_new, p_out), (m_new, m_out), (v_new, v_out)]
    started = [
        pltpu.make_async_copy(src, dst, sem.at[i]) for i, (src, dst) in enumerate(copies)
    ]
    for copy in started:
        copy.start()
    for copy in started:
        copy.wait()


def on_device(params, gradient, first_moment, second_moment):
    rows, width = params.shape
    entries = rows * width * lax.axis_size("group") * lax.axis_size("shard")
    whole = (rows * lax.axis_size("shard"), width)
    f32, bf16 = jnp.float32, jnp.bfloat16
    messages = 4 * (NX * NZ - 1)
    hbm = pl.BlockSpec(memory_space=pltpu.HBM)
    vmem = pl.BlockSpec(memory_space=pltpu.VMEM)
    rep, p_new, m_new, v_new = pl.pallas_call(
        functools.partial(step_kernel, entries),
        out_shape=(
            pltpu.VMEM(whole, bf16),
            pltpu.VMEM((rows, width), f32),
            pltpu.VMEM((rows, width), f32),
            pltpu.VMEM((rows, width), f32),
        ),
        in_specs=[hbm] * 4,
        out_specs=[vmem] * 4,
        scratch_shapes=[
            pltpu.VMEM((rows, width), f32),
            pltpu.VMEM((rows, width), bf16),
            pltpu.VMEM((rows, width), f32),
            pltpu.VMEM((rows, width), f32),
            pltpu.VMEM((NG, 1, LANES), f32),
            pltpu.VMEM((NX, 1, LANES), f32),
            pltpu.VMEM((NZ, 1, LANES), f32),
            pltpu.SemaphoreType.DMA((4,)),
            pltpu.SemaphoreType.DMA((NG + NX + NZ - 3,)),
            pltpu.SemaphoreType.DMA((NG + NX + NZ - 3,)),
            pltpu.SemaphoreType.DMA((messages,)),
            pltpu.SemaphoreType.DMA((messages,)),
        ],
        compiler_params=pltpu.CompilerParams(
            collective_id=0, has_side_effects=True, vmem_limit_bytes=58_200_000
        ),
        name="step",
    )(params, gradient, first_moment, second_moment)
    return pl.pallas_call(
        store_kernel,
        out_shape=(
            jax.ShapeDtypeStruct((rows, width), f32),
            jax.ShapeDtypeStruct((rows, width), f32),
            jax.ShapeDtypeStruct((rows, width), f32),
            jax.ShapeDtypeStruct(whole, bf16),
        ),
        in_specs=[vmem] * 4,
        out_specs=[hbm] * 4,
        scratch_shapes=[pltpu.SemaphoreType.DMA((11,))],
        compiler_params=pltpu.CompilerParams(vmem_limit_bytes=24 * 2**20),
        name="store",
    )(rep, p_new, m_new, v_new)


def solution(mesh):
    rows = P(("group", "shard"), None)
    return jax.shard_map(
        on_device,
        mesh=mesh,
        in_specs=(rows,) * 4,
        out_specs=(rows, rows, rows, P("group", None)),
        check_vma=False,
    )
```

time: 145 us -> 69.9 us (0.48)
  waiting for transfers between devices: 86.6 us -> 0 us
  Pallas kernels: 0 us -> 69.1 us
  blocking collectives: 29.5 us -> 0 us
  between operations: 14.7 us -> 0.64 us
  local copies, waits for them, and re-layouts: 7.9 us -> 0 us
  other arithmetic: 5.71 us -> 0 us
    all_gather x1 -> x0, waiting for transfers between devices: 86.6 us -> none  [on_device(): replica = lax.all_gather(rounded, 'shard', axis=0, tiled=True)]
    pallas_call x0 -> x2, Pallas kernels: none -> 69.1 us  [the longest x1 65.6 us: on_device(): pl.pallas_call(functools.partial(step_kernel, entries), out_shape=(pltpu....]
    all_to_all x2 -> x0, blocking collectives: 29.5 us -> none  [copy_for_each(): return lax.all_to_all(copies, axis, split_axis=0, concat_axis=0, tiled=True)]
    unnamed x1 -> x0, local copies, waits for them, and re-layouts: 6.6 us -> none
    reduce_sum x3 -> x0, other arithmetic: 2.91 us -> none  [the longest x1 1.66 us: on_device(): local_sum = jnp.sum(grad_local * grad_local)]
    convert_element_type x1 -> x0, other arithmetic: 2.8 us -> none  [advance_rows(): return (new_params, new_first, new_second, new_params.astype(jnp.bfloat16))]
  transfers between devices with their start and end apart: 1 -> 0, of which waited for: 1 -> 0; matrix products, arithmetic and copies ran while one was open for 0% -> 0% of each run, Pallas kernels for 0% -> 0%
where the time goes in v1:
time: 69.9 us; the launch traced here: 69.7 us
  Pallas kernels  69.1 us (99%)
    pallas_call x1, Pallas kernels, on_device(): pl.pallas_call(functools.partial(step_kernel, entries), out_shape=(pltpu....  65.6 us
    pallas_call x1, Pallas kernels, on_device(): pl.pallas_call(store_kernel, out_shape=(jax.ShapeDtypeStruct((rows, width...  3.48 us

profile of v1, /device:TPU:8, one launch (start us, length us, event | category | flops | bytes accessed | tf_op | source)
XLA Modules:
  0.0 69.7 jit_solution(13024240715238787396)
XLA Ops:
  0.6 65.6 %step.1 = (bf16[512,7168]{1,0:T(8,128)(2,1)S(1)}, f32[16,7168]{1,0:T(8,128)S(1)}, f32[16,7168]{1,0:T(8,128)S(1)}, f32[16,7168]{1,0:T(8,128)S(1)}) custom-call(f32[16,7168]{1,0:T(8,128)} %p_hbm.1, bf16[16,7168]{1,0:T(8,128)(2,1)} %g_hbm.1, f32[16,7168]{1,0:T(8,128)} %m_hbm.1, f32[16,7168]{1,0:T(8,128)} %v_hbm.1), custom_call_target="tpu_custom_call" | custom-call | tf_op jit(solution)/shard_map/step/pallas_call | solution.py:253
  66.2 3.5 %store.1 = (f32[16,7168]{1,0:T(8,128)}, f32[16,7168]{1,0:T(8,128)}, f32[16,7168]{1,0:T(8,128)}, bf16[512,7168]{1,0:T(8,128)(2,1)}) custom-call(bf16[512,7168]{1,0:T(8,128)(2,1)S(1)} %get-tuple-element.8.rep, f32[16,7168]{1,0:T(8,128)S(1)} %get-tuple-element.9.p_new, f32[16,7168]{1,0:T(8,128)S(1)} %get-tuple-element.10.m_new, ...), custom_call_target="tpu_custom_call" | custom-call | tf_op jit(solution)/shard_map/store/pallas_call | solution.py:282

commit v2 on v1

--- a/solution.py
+++ b/solution.py
@@ -49,27 +49,42 @@
     return sends
 
 
-def order_of(pieces, sends, rate=46.6e3, latency=1.5):
+def plan_of(pieces, sends, rate=46.6e3, latency=1.8, ahead=1.5):
+    @functools.cache
+    def depth(place):
+        return max((1 + depth(there) for *_, there in sends.get(place, ())), default=0)
+
     queues = {link: [] for link in itertools.product("xz", (1, -1))}
     free = dict.fromkeys(queues, 0.0)
     count = itertools.count()
-    events = [(0.02 * v, next(count), (v, 0, 0)) for v in range(len(pieces))]
-    events += [(0.0, next(count), None)]
-    heapq.heapify(events)
-    order = []
+    events = [(0.15 * v, next(count), (v, 0, 0)) for v in range(len(pieces))]
+    steps, held, turns = [], {}, []
     while events:
-        now, _, place = heapq.heappop(events)
-        if place is not None:
-            order.append(place)
-            for axis, step, there in sends.get(place, ()):
-                queues[axis, step].append(there)
+        now = events[0][0]
+        while events and events[0][0] <= now + 1e-9:
+            _, _, place = heapq.heappop(events)
+            if place is not None:
+                for axis, step, there in sends.get(place, ()):
+                    heapq.heappush(
+                        queues[axis, step], (-depth(there), next(count), there)
+                    )
+                    held[there] = len(steps)
+                steps.append((now, place, []))
         for link, queue in queues.items():
             if queue and free[link] <= now + 1e-9:
-                there = queue.pop(0)
+                _, _, there = heapq.heappop(queue)
                 free[link] = now + pieces[there[0]][2] * ROWS * 2 / rate
                 heapq.heappush(events, (free[link], next(count), None))
                 heapq.heappush(events, (free[link] + latency, next(count), there))
-    return [place for place in order if place[1:] != (0, 0)]
+                turns.append((now, link, there))
+    last = dict.fromkeys(queues, 0)
+    for turn, link, there in turns:
+        i = held[there]
+        while i + 1 < len(steps) and steps[i + 1][0] <= turn - ahead:
+            i += 1
+        last[link] = max(i, last[link])
+        steps[last[link]][2].append((*link, there))
+    return [(place, starts) for _, place, starts in steps]
 
 
 def step_kernel(
@@ -86,8 +101,7 @@
     g_in,
     m_in,
     v_in,
-    y_buf,
-    x_buf,
+    plane_buf,
     z_buf,
     load_sem,
     sum_send,
@@ -100,11 +114,9 @@
     shard = lax.axis_index("shard")
     x, z = shard // NZ, shard % NZ
 
-    def at_group(k):
-        return ((group + k) % NG, shard)
-
-    def at(dx, dz):
-        return (group, (x + dx + NX) % NX * NZ + (z + dz + NZ) % NZ)
+    def at(dx, dz, dg=0):
+        to = (x + dx + NX) % NX * NZ + (z + dz + NZ) % NZ
+        return ((group + dg) % NG, to)
 
     loads = [
         pltpu.make_async_copy(src, dst, load_sem.at[i])
@@ -116,13 +128,12 @@
         load.start()
 
     stages = (
-        (y_buf, [at_group(k) for k in range(1, NG)]),
-        (x_buf, [at(k, 0) for k in range(1, NX)]),
+        (plane_buf, [at(k // NG, 0, k % NG) for k in range(1, NX * NG)]),
         (z_buf, [at(0, k) for k in range(1, NZ)]),
     )
     barrier = pltpu.get_barrier_semaphore()
     peers = [peer for _, those in stages for peer in those]
-    for peer in peers:
+    for peer in reversed(peers):
         pl.semaphore_signal(barrier, inc=1, device_id=peer, device_id_type=MESH)
 
     loads[0].wait()
@@ -133,30 +144,27 @@
     total = jnp.sum(total, axis=0, keepdims=True)
 
     pl.semaphore_wait(barrier, len(peers))
-    sent = []
-    base = 0
-    for buf, those in stages:
+    summed = []
+    for i, (buf, those) in enumerate(stages):
         buf[0] = total
-        copies = [
-            pltpu.make_async_remote_copy(
-                src_ref=buf.at[0],
-                dst_ref=buf.at[k],
-                send_sem=sum_send.at[base + k - 1],
-                recv_sem=sum_recv.at[base + k - 1],
+
+        def message(src, dst, peer):
+            return pltpu.make_async_remote_copy(
+                src_ref=buf.at[src],
+                dst_ref=buf.at[dst],
+                send_sem=sum_send.at[i],
+                recv_sem=sum_recv.at[i],
                 device_id=peer,
                 device_id_type=MESH,
             )
-            for k, peer in enumerate(those, 1)
-        ]
-        for copy in copies:
-            copy.start()
-        for copy in copies:
-            copy.wait_recv()
-        total = buf[0]
-        for k in range(1, len(those) + 1):
-            total = total + buf[k]
-        sent += copies
-        base += len(those)
+
+        for k, peer in enumerate(those, 1):
+            message(0, k, peer).start()
+        others = pl.ds(1, len(those))
+        every = message(others, others, those[0])
+        every.wait_recv()
+        summed.append(every)
+        total = jnp.sum(buf[...], axis=0)
 
     norm_total = jnp.sum(total, axis=1, keepdims=True)
     scale = jnp.minimum(1.0, 1.0 / jnp.sqrt(norm_total / entries + 1e-06))
@@ -165,8 +173,13 @@
 
     pieces = pieces_of(width)
     sends = trees_of(pieces)
-    order = order_of(pieces, sends)
-    slot = {place: i for i, place in enumerate(order)}
+    plan = plan_of(pieces, sends)
+    ends = [place for place, _ in plan if place not in sends]
+    waits = [place for place, _ in plan[len(pieces) :] if place in sends]
+    slot = {place: i for i, place in enumerate(waits)}
+    sizes = sorted({piece[1:3] for piece in pieces})
+    for place in ends:
+        slot[place] = len(waits) + sizes.index(pieces[place[0]][1:3])
 
     def view(place):
         v, ox, oz = place
@@ -181,17 +194,15 @@
         return pltpu.make_async_remote_copy(
             src_ref=view(here),
             dst_ref=view(here),
-            send_sem=send_sem.at[slot[there]],
+            send_sem=send_sem.at[0],
             recv_sem=recv_sem.at[slot[there]],
             device_id=at(step, 0) if axis == "x" else at(0, step),
             device_id_type=MESH,
         )
 
-    def forward(place):
-        for axis, step, there in sends.get(place, ()):
-            copy = copy_to(axis, step, there)
-            copy.start()
-            sent.append(copy)
+    def start(starts):
+        for axis, step, there in starts:
+            copy_to(axis, step, there).start()
 
     correct_one = 1.0 - 0.9**10
     correct_two = 1.0 - 0.95**10
@@ -213,16 +224,37 @@
             m_out[rows, cols] = new_first
             v_out[rows, cols] = new_second
             rep[pl.ds(mine + row, ROWS), cols] = new_params.astype(jnp.bfloat16)
-        forward((v, 0, 0))
+        start(plan[v][1])
 
     arrival = {
         there: (axis, step) for those in sends.values() for axis, step, there in those
     }
-    for place in order:
-        copy_to(*arrival[place], place).wait_recv()
-        forward(place)
-    for copy in sent:
-        copy.wait_send()
+    for place, starts in plan[len(pieces) :]:
+        if place in sends:
+            copy_to(*arrival[place], place).wait_recv()
+        start(starts)
+    sent = rep.at[pl.ds(0, rep.shape[0] - 16)]
+    pltpu.make_async_remote_copy(
+        src_ref=sent,
+        dst_ref=sent,
+        send_sem=send_sem.at[0],
+        recv_sem=recv_sem.at[0],
+        device_id=at(1, 0),
+        device_id_type=MESH,
+    ).wait_send()
+    for every in summed:
+        every.wait_send()
+    for i, (column, columns) in enumerate(sizes):
+        these = [place for place in ends if pieces[place[0]][1] == column]
+        taken = rep.at[pl.ds(0, len(these) * ROWS), pl.ds(column, columns)]
+        pltpu.make_async_remote_copy(
+            src_ref=taken,
+            dst_ref=taken,
+            send_sem=send_sem.at[0],
+            recv_sem=recv_sem.at[len(waits) + i],
+            device_id=at(1, 0),
+            device_id_type=MESH,
+        ).wait_recv()
 
 
 def store_kernel(rep, p_new, m_new, v_new, p_out, m_out, v_out, rep_out, sem):
@@ -247,7 +279,7 @@
     entries = rows * width * lax.axis_size("group") * lax.axis_size("shard")
     whole = (rows * lax.axis_size("shard"), width)
     f32, bf16 = jnp.float32, jnp.bfloat16
-    messages = 4 * (NX * NZ - 1)
+    messages = 78
     hbm = pl.BlockSpec(memory_space=pltpu.HBM)
     vmem = pl.BlockSpec(memory_space=pltpu.VMEM)
     rep, p_new, m_new, v_new = pl.pallas_call(
@@ -265,13 +297,12 @@
             pltpu.VMEM((rows, width), bf16),
             pltpu.VMEM((rows, width), f32),
             pltpu.VMEM((rows, width), f32),
-            pltpu.VMEM((NG, 1, LANES), f32),
-            pltpu.VMEM((NX, 1, LANES), f32),
+            pltpu.VMEM((NX * NG, 1, LANES), f32),
             pltpu.VMEM((NZ, 1, LANES), f32),
             pltpu.SemaphoreType.DMA((4,)),
-            pltpu.SemaphoreType.DMA((NG + NX + NZ - 3,)),
-            pltpu.SemaphoreType.DMA((NG + NX + NZ - 3,)),
-            pltpu.SemaphoreType.DMA((messages,)),
+            pltpu.SemaphoreType.DMA((2,)),
+            pltpu.SemaphoreType.DMA((2,)),
+            pltpu.SemaphoreType.DMA((1,)),
             pltpu.SemaphoreType.DMA((messages,)),
         ],
         compiler_params=pltpu.CompilerParams(

time: 69.9 us -> 63.9 us (0.914)
  Pallas kernels: 69.1 us -> 63.1 us
    pallas_call x1, Pallas kernels: 65.6 us -> 59.6 us  [on_device(): pl.pallas_call(functools.partial(step_kernel, entries), out_shape=(pltpu....]
where the time goes in v2:
time: 63.9 us; the launch traced here: 63.8 us
  Pallas kernels  63.1 us (99%)
  between operations  0.64 us (1%)
    pallas_call x1, Pallas kernels, on_device(): pl.pallas_call(functools.partial(step_kernel, entries), out_shape=(pltpu....  59.6 us
    pallas_call x1, Pallas kernels, on_device(): pl.pallas_call(store_kernel, out_shape=(jax.ShapeDtypeStruct((rows, width...  3.48 us

profile of v2, /device:TPU:8, one launch (start us, length us, event | category | flops | bytes accessed | tf_op | source)
XLA Modules:
  0.0 63.8 jit_solution(3682928238381872227)
XLA Ops:
  0.6 59.6 %step.1 = (bf16[512,7168]{1,0:T(8,128)(2,1)S(1)}, f32[16,7168]{1,0:T(8,128)S(1)}, f32[16,7168]{1,0:T(8,128)S(1)}, f32[16,7168]{1,0:T(8,128)S(1)}) custom-call(f32[16,7168]{1,0:T(8,128)} %p_hbm.1, bf16[16,7168]{1,0:T(8,128)(2,1)} %g_hbm.1, f32[16,7168]{1,0:T(8,128)} %m_hbm.1, f32[16,7168]{1,0:T(8,128)} %v_hbm.1), custom_call_target="tpu_custom_call" | custom-call | tf_op jit(solution)/shard_map/step/pallas_call | solution.py:285
  60.3 3.5 %store.1 = (f32[16,7168]{1,0:T(8,128)}, f32[16,7168]{1,0:T(8,128)}, f32[16,7168]{1,0:T(8,128)}, bf16[512,7168]{1,0:T(8,128)(2,1)}) custom-call(bf16[512,7168]{1,0:T(8,128)(2,1)S(1)} %get-tuple-element.8.rep, f32[16,7168]{1,0:T(8,128)S(1)} %get-tuple-element.9.p_new, f32[16,7168]{1,0:T(8,128)S(1)} %get-tuple-element.10.m_new, ...), custom_call_target="tpu_custom_call" | custom-call | tf_op jit(solution)/shard_map/store/pallas_call | solution.py:313

commit v3 on v2

--- a/solution.py
+++ b/solution.py
@@ -10,7 +10,7 @@
 from jax.sharding import PartitionSpec as P
 
 MESH = pl.DeviceIdType.MESH
-NG, NX, NZ = 8, 4, 8
+NY, NX, NZ = 4, 4, 8
 LANES = 128
 ROWS = 8
 
@@ -49,7 +49,7 @@
     return sends
 
 
-def plan_of(pieces, sends, rate=46.6e3, latency=1.8, ahead=1.5):
+def plan_of(pieces, sends, rate=46.6e3, latency=2.4, ahead=1.5):
     @functools.cache
     def depth(place):
         return max((1 + depth(there) for *_, there in sends.get(place, ())), default=0)
@@ -87,6 +87,39 @@
     return [(place, starts) for _, place, starts in steps]
 
 
+def source_of(send):
+    axis, step, (v, ox, oz) = send
+    return (v, ox - step, oz) if axis == "x" else (v, ox, oz - step)
+
+
+def waits_of(pieces, sends, plan):
+    there_by = {place: i for i, (place, _) in enumerate(plan)}
+    needed = {}
+    for i, (_, starts) in enumerate(plan):
+        for send in starts:
+            needed.setdefault(source_of(send), i)
+    waits = [[] for _ in range(len(plan) + 1)]
+    for size in sorted({piece[1:3] for piece in pieces}):
+        left = sorted(
+            (needed.get(place, len(plan)), i, place)
+            for place, i in there_by.items()
+            if i >= len(pieces) and pieces[place[0]][1:3] == size
+        )
+        while left:
+            at = left[0][0]
+            waits[at].append([place for _, i, place in left if i <= at])
+            left = [entry for entry in left if entry[1] > at]
+    return waits
+
+
+def far_first(offsets):
+    def chips(to):
+        sizes = (NX, NZ, NY)
+        return sum(min(step, size - step) for step, size in zip(to, sizes))
+
+    return sorted(offsets, key=chips, reverse=True)
+
+
 def step_kernel(
     entries,
     p_hbm,
@@ -101,8 +134,10 @@
     g_in,
     m_in,
     v_in,
+    own_buf,
     plane_buf,
     z_buf,
+    all_buf,
     load_sem,
     sum_send,
     sum_recv,
@@ -114,9 +149,12 @@
     shard = lax.axis_index("shard")
     x, z = shard // NZ, shard % NZ
 
-    def at(dx, dz, dg=0):
+    y, core = group // 2, group % 2
+    hub = core == 1
+
+    def at(dx, dz, dy=0, to_core=core):
         to = (x + dx + NX) % NX * NZ + (z + dz + NZ) % NZ
-        return ((group + dg) % NG, to)
+        return ((y + dy + NY) % NY * 2 + to_core, to)
 
     loads = [
         pltpu.make_async_copy(src, dst, load_sem.at[i])
@@ -124,47 +162,89 @@
             ((g_hbm, g_in), (p_hbm, p_in), (m_hbm, m_in), (v_hbm, v_in))
         )
     ]
-    for load in loads:
+    loads[0].start()
+
+    plane = far_first((dx, 0, dy) for dx in range(NX) for dy in range(NY))
+    line = far_first((0, dz, 0) for dz in range(NZ))
+    near = ((1, 0), (-1, 0), (0, 1), (0, -1))
+    barrier = pltpu.get_barrier_semaphore()
+
+    def greet(peer):
+        pl.semaphore_signal(barrier, inc=1, device_id=peer, device_id_type=MESH)
+
+    @pl.when(hub)
+    def _():
+        for to in (*line[:-1], *plane[:-1]):
+            greet(at(*to, 1))
+        for to in plane:
+            greet(at(*to, 0))
+
+    @pl.when(~hub)
+    def _():
+        for to in near:
+            greet(at(*to))
+        greet(at(0, 0, 0, 1))
+
+    loads[0].wait()
+    for load in loads[1:]:
         load.start()
-
-    stages = (
-        (plane_buf, [at(k // NG, 0, k % NG) for k in range(1, NX * NG)]),
-        (z_buf, [at(0, k) for k in range(1, NZ)]),
-    )
-    barrier = pltpu.get_barrier_semaphore()
-    peers = [peer for _, those in stages for peer in those]
-    for peer in reversed(peers):
-        pl.semaphore_signal(barrier, inc=1, device_id=peer, device_id_type=MESH)
-
-    loads[0].wait()
     total = jnp.zeros((16, LANES), jnp.float32)
     for c in range(0, width, LANES):
         part = g_in[:, c : c + LANES].astype(jnp.float32)
         total = total + part * part
     total = jnp.sum(total, axis=0, keepdims=True)
 
-    pl.semaphore_wait(barrier, len(peers))
-    summed = []
-    for i, (buf, those) in enumerate(stages):
-        buf[0] = total
-
-        def message(src, dst, peer):
-            return pltpu.make_async_remote_copy(
-                src_ref=buf.at[src],
-                dst_ref=buf.at[dst],
-                send_sem=sum_send.at[i],
-                recv_sem=sum_recv.at[i],
-                device_id=peer,
-                device_id_type=MESH,
-            )
-
-        for k, peer in enumerate(those, 1):
-            message(0, k, peer).start()
-        others = pl.ds(1, len(those))
-        every = message(others, others, those[0])
-        every.wait_recv()
-        summed.append(every)
-        total = jnp.sum(buf[...], axis=0)
+    own_buf[0] = total
+
+    @pl.when(hub)
+    def _():
+        plane_buf[0] = total
+        pl.semaphore_wait(barrier, len(plane) + len(line) - 1)
+
+    @pl.when(~hub)
+    def _():
+        pl.semaphore_wait(barrier, len(plane) + len(near))
+
+    def message(stage, src, dst, peer):
+        return pltpu.make_async_remote_copy(
+            src_ref=src,
+            dst_ref=dst,
+            send_sem=sum_send.at[stage],
+            recv_sem=sum_recv.at[stage],
+            device_id=peer,
+            device_id_type=MESH,
+        )
+
+    def part_to(to):
+        place = (to[0] * NY + to[2]) * 2 + 1 - core
+        return message(0, own_buf.at[0], plane_buf.at[place], at(*to, 1))
+
+    def several(stage, count):
+        those = plane_buf.at[pl.ds(0, count)]
+        return message(stage, those, those, at(1, 0))
+
+    for to in plane[:-1]:
+        part_to(to).start()
+
+    @pl.when(~hub)
+    def _():
+        part_to(plane[-1]).start()
+
+    @pl.when(hub)
+    def _():
+        several(0, 2 * len(plane) - 1).wait_recv()
+        z_buf[0] = jnp.sum(plane_buf[...], axis=0)
+        for to in line[:-1]:
+            message(1, z_buf.at[0], z_buf.at[to[1]], at(*to, 1)).start()
+        several(1, len(line) - 1).wait_recv()
+        all_buf[0] = jnp.sum(z_buf[...], axis=0)
+        message(1, all_buf.at[0], all_buf.at[0], at(0, 0, 0, 0)).start()
+
+    @pl.when(~hub)
+    def _():
+        several(1, 1).wait_recv()
+
+    total = all_buf[0]
 
     norm_total = jnp.sum(total, axis=1, keepdims=True)
     scale = jnp.minimum(1.0, 1.0 / jnp.sqrt(norm_total / entries + 1e-06))
@@ -174,12 +254,9 @@
     pieces = pieces_of(width)
     sends = trees_of(pieces)
     plan = plan_of(pieces, sends)
-    ends = [place for place, _ in plan if place not in sends]
-    waits = [place for place, _ in plan[len(pieces) :] if place in sends]
-    slot = {place: i for i, place in enumerate(waits)}
-    sizes = sorted({piece[1:3] for piece in pieces})
-    for place in ends:
-        slot[place] = len(waits) + sizes.index(pieces[place[0]][1:3])
+    waits = waits_of(pieces, sends, plan)
+    groups = [group for those in waits for group in those]
+    slot = {place: i for i, group in enumerate(groups) for place in group}
 
     def view(place):
         v, ox, oz = place
@@ -188,21 +265,25 @@
         start = pl.multiple_of(source * 16 + row, 8)
         return rep.at[pl.ds(start, ROWS), pl.ds(column, columns)]
 
-    def copy_to(axis, step, there):
-        v, ox, oz = there
-        here = (v, ox - step, oz) if axis == "x" else (v, ox, oz - step)
+    def copy_of(ref, index, peer):
         return pltpu.make_async_remote_copy(
-            src_ref=view(here),
-            dst_ref=view(here),
+            src_ref=ref,
+            dst_ref=ref,
             send_sem=send_sem.at[0],
-            recv_sem=recv_sem.at[slot[there]],
-            device_id=at(step, 0) if axis == "x" else at(0, step),
+            recv_sem=recv_sem.at[index],
+            device_id=peer,
             device_id_type=MESH,
         )
 
-    def start(starts):
-        for axis, step, there in starts:
-            copy_to(axis, step, there).start()
+    def run(step):
+        for group in waits[step]:
+            _, column, columns, *_ = pieces[group[0][0]]
+            taken = rep.at[pl.ds(0, len(group) * ROWS), pl.ds(column, columns)]
+            copy_of(taken, slot[group[0]], at(1, 0)).wait_recv()
+        for send in plan[step][1] if step < len(plan) else ():
+            axis, way, there = send
+            peer = at(way, 0) if axis == "x" else at(0, way)
+            copy_of(view(source_of(send)), slot[there], peer).start()
 
     correct_one = 1.0 - 0.9**10
     correct_two = 1.0 - 0.95**10
@@ -224,37 +305,20 @@
             m_out[rows, cols] = new_first
             v_out[rows, cols] = new_second
             rep[pl.ds(mine + row, ROWS), cols] = new_params.astype(jnp.bfloat16)
-        start(plan[v][1])
-
-    arrival = {
-        there: (axis, step) for those in sends.values() for axis, step, there in those
-    }
-    for place, starts in plan[len(pieces) :]:
-        if place in sends:
-            copy_to(*arrival[place], place).wait_recv()
-        start(starts)
+        run(v)
+
+    for i in range(len(pieces), len(plan) + 1):
+        run(i)
     sent = rep.at[pl.ds(0, rep.shape[0] - 16)]
-    pltpu.make_async_remote_copy(
-        src_ref=sent,
-        dst_ref=sent,
-        send_sem=send_sem.at[0],
-        recv_sem=recv_sem.at[0],
-        device_id=at(1, 0),
-        device_id_type=MESH,
-    ).wait_send()
-    for every in summed:
-        every.wait_send()
-    for i, (column, columns) in enumerate(sizes):
-        these = [place for place in ends if pieces[place[0]][1] == column]
-        taken = rep.at[pl.ds(0, len(these) * ROWS), pl.ds(column, columns)]
-        pltpu.make_async_remote_copy(
-            src_ref=taken,
-            dst_ref=taken,
-            send_sem=send_sem.at[0],
-            recv_sem=recv_sem.at[len(waits) + i],
-            device_id=at(1, 0),
-            device_id_type=MESH,
-        ).wait_recv()
+    copy_of(sent, 0, at(1, 0)).wait_send()
+    @pl.when(hub)
+    def _():
+        several(0, len(plane) - 1).wait_send()
+        several(1, len(line)).wait_send()
+
+    @pl.when(~hub)
+    def _():
+        several(0, len(plane)).wait_send()
 
 
 def store_kernel(rep, p_new, m_new, v_new, p_out, m_out, v_out, rep_out, sem):
@@ -279,7 +343,10 @@
     entries = rows * width * lax.axis_size("group") * lax.axis_size("shard")
     whole = (rows * lax.axis_size("shard"), width)
     f32, bf16 = jnp.float32, jnp.bfloat16
-    messages = 78
+    pieces = pieces_of(width)
+    sends = trees_of(pieces)
+    waits = waits_of(pieces, sends, plan_of(pieces, sends))
+    messages = sum(len(groups) for groups in waits)
     hbm = pl.BlockSpec(memory_space=pltpu.HBM)
     vmem = pl.BlockSpec(memory_space=pltpu.VMEM)
     rep, p_new, m_new, v_new = pl.pallas_call(
@@ -297,8 +364,10 @@
             pltpu.VMEM((rows, width), bf16),
             pltpu.VMEM((rows, width), f32),
             pltpu.VMEM((rows, width), f32),
-            pltpu.VMEM((NX * NG, 1, LANES), f32),
+            pltpu.VMEM((1, 1, LANES), f32),
+            pltpu.VMEM((NX * NY * 2, 1, LANES), f32),
             pltpu.VMEM((NZ, 1, LANES), f32),
+            pltpu.VMEM((1, 1, LANES), f32),
             pltpu.SemaphoreType.DMA((4,)),
             pltpu.SemaphoreType.DMA((2,)),
             pltpu.SemaphoreType.DMA((2,)),

time: 63.9 us -> 62.1 us (0.972)
  Pallas kernels: 63.1 us -> 61.1 us
    pallas_call x1, Pallas kernels: 59.6 us -> 57.6 us  [on_device(): pl.pallas_call(functools.partial(step_kernel, entries), out_shape=(pltpu....]
where the time goes in v3:
time: 62.1 us; the launch traced here: 61.7 us
  Pallas kernels  61.1 us (98%)
  between operations  0.64 us (1%)
    pallas_call x1, Pallas kernels, on_device(): pl.pallas_call(functools.partial(step_kernel, entries), out_shape=(pltpu....  57.6 us
    pallas_call x1, Pallas kernels, on_device(): pl.pallas_call(store_kernel, out_shape=(jax.ShapeDtypeStruct((rows, width...  3.48 us

profile of v3, /device:TPU:8, one launch (start us, length us, event | category | flops | bytes accessed | tf_op | source)
XLA Modules:
  0.0 61.7 jit_solution(6188693883580640064)
XLA Ops:
  0.6 57.6 %step.1 = (bf16[512,7168]{1,0:T(8,128)(2,1)S(1)}, f32[16,7168]{1,0:T(8,128)S(1)}, f32[16,7168]{1,0:T(8,128)S(1)}, f32[16,7168]{1,0:T(8,128)S(1)}) custom-call(f32[16,7168]{1,0:T(8,128)} %p_hbm.1, bf16[16,7168]{1,0:T(8,128)(2,1)} %g_hbm.1, f32[16,7168]{1,0:T(8,128)} %m_hbm.1, f32[16,7168]{1,0:T(8,128)} %v_hbm.1), custom_call_target="tpu_custom_call" | custom-call | tf_op jit(solution)/shard_map/step/pallas_call | solution.py:352
  58.2 3.5 %store.1 = (f32[16,7168]{1,0:T(8,128)}, f32[16,7168]{1,0:T(8,128)}, f32[16,7168]{1,0:T(8,128)}, bf16[512,7168]{1,0:T(8,128)(2,1)}) custom-call(bf16[512,7168]{1,0:T(8,128)(2,1)S(1)} %get-tuple-element.8.rep, f32[16,7168]{1,0:T(8,128)S(1)} %get-tuple-element.9.p_new, f32[16,7168]{1,0:T(8,128)S(1)} %get-tuple-element.10.m_new, ...), custom_call_target="tpu_custom_call" | custom-call | tf_op jit(solution)/shard_map/store/pallas_call | solution.py:382

commit v4 on v3

--- a/solution.py
+++ b/solution.py
@@ -49,10 +49,14 @@
     return sends
 
 
-def plan_of(pieces, sends, rate=46.6e3, latency=2.4, ahead=1.5):
+def plan_of(pieces, sends, rate=46.6e3, latency=2.4, ahead=2.0):
     @functools.cache
     def depth(place):
         return max((1 + depth(there) for *_, there in sends.get(place, ())), default=0)
+
+    @functools.cache
+    def size(place):
+        return 1 + sum(size(there) for *_, there in sends.get(place, ()))
 
     queues = {link: [] for link in itertools.product("xz", (1, -1))}
     free = dict.fromkeys(queues, 0.0)
@@ -66,13 +70,13 @@
             if place is not None:
                 for axis, step, there in sends.get(place, ()):
                     heapq.heappush(
-                        queues[axis, step], (-depth(there), next(count), there)
+                        queues[axis, step], (-depth(there), -size(there), next(count), there)
                     )
                     held[there] = len(steps)
                 steps.append((now, place, []))
         for link, queue in queues.items():
             if queue and free[link] <= now + 1e-9:
-                _, _, there = heapq.heappop(queue)
+                *_, there = heapq.heappop(queue)
                 free[link] = now + pieces[there[0]][2] * ROWS * 2 / rate
                 heapq.heappush(events, (free[link], next(count), None))
                 heapq.heappush(events, (free[link] + latency, next(count), there))
@@ -322,20 +326,18 @@
 
 
 def store_kernel(rep, p_new, m_new, v_new, p_out, m_out, v_out, rep_out, sem):
-    parts = 8
+    parts = 4
     rows = rep.shape[0] // parts
     copies = [
         (rep.at[pl.ds(i * rows, rows)], rep_out.at[pl.ds(i * rows, rows)])
         for i in range(parts)
     ]
     copies += [(p_new, p_out), (m_new, m_out), (v_new, v_out)]
-    started = [
-        pltpu.make_async_copy(src, dst, sem.at[i]) for i, (src, dst) in enumerate(copies)
-    ]
-    for copy in started:
-        copy.start()
-    for copy in started:
-        copy.wait()
+    for i, (src, dst) in enumerate(copies):
+        pltpu.make_async_copy(src, dst, sem.at[max(i - parts + 1, 0)]).start()
+    whole = [(rep, rep_out), *copies[parts:]]
+    for i, (src, dst) in enumerate(whole):
+        pltpu.make_async_copy(src, dst, sem.at[i]).wait()
 
 
 def on_device(params, gradient, first_moment, second_moment):
@@ -389,7 +391,7 @@
         ),
         in_specs=[vmem] * 4,
         out_specs=[hbm] * 4,
-        scratch_shapes=[pltpu.SemaphoreType.DMA((11,))],
+        scratch_shapes=[pltpu.SemaphoreType.DMA((4,))],
         compiler_params=pltpu.CompilerParams(vmem_limit_bytes=24 * 2**20),
         name="store",
     )(rep, p_new, m_new, v_new)

time: 62.1 us -> 62.1 us (level)
  no operation moved by 1% of the time
where the time goes in v4:
time: 62.1 us; the launch traced here: 61.6 us
  Pallas kernels  60.9 us (98%)
  between operations  0.64 us (1%)
    pallas_call x1, Pallas kernels, on_device(): pl.pallas_call(functools.partial(step_kernel, entries), out_shape=(pltpu....  57.5 us
    pallas_call x1, Pallas kernels, on_device(): pl.pallas_call(store_kernel, out_shape=(jax.ShapeDtypeStruct((rows, width...  3.44 us

profile of v4, /device:TPU:8, one launch (start us, length us, event | category | flops | bytes accessed | tf_op | source)
XLA Modules:
  0.0 61.6 jit_solution(2621972946921493938)
XLA Ops:
  0.6 57.5 %step.1 = (bf16[512,7168]{1,0:T(8,128)(2,1)S(1)}, f32[16,7168]{1,0:T(8,128)S(1)}, f32[16,7168]{1,0:T(8,128)S(1)}, f32[16,7168]{1,0:T(8,128)S(1)}) custom-call(f32[16,7168]{1,0:T(8,128)} %p_hbm.1, bf16[16,7168]{1,0:T(8,128)(2,1)} %g_hbm.1, f32[16,7168]{1,0:T(8,128)} %m_hbm.1, f32[16,7168]{1,0:T(8,128)} %v_hbm.1), custom_call_target="tpu_custom_call" | custom-call | tf_op jit(solution)/shard_map/step/pallas_call | solution.py:354
  58.1 3.4 %store.1 = (f32[16,7168]{1,0:T(8,128)}, f32[16,7168]{1,0:T(8,128)}, f32[16,7168]{1,0:T(8,128)}, bf16[512,7168]{1,0:T(8,128)(2,1)}) custom-call(bf16[512,7168]{1,0:T(8,128)(2,1)S(1)} %get-tuple-element.8.rep, f32[16,7168]{1,0:T(8,128)S(1)} %get-tuple-element.9.p_new, f32[16,7168]{1,0:T(8,128)S(1)} %get-tuple-element.10.m_new, ...), custom_call_target="tpu_custom_call" | custom-call | tf_op jit(solution)/shard_map/store/pallas_call | solution.py:384

commit v5 on v4

--- a/solution.py
+++ b/solution.py
@@ -16,12 +16,12 @@
 
 
 def pieces_of(width):
-    cut = (width // LANES * 23 // 56) * LANES
+    upper, lower = (width // LANES * part // 56 * LANES for part in (23, 22))
     return (
-        (0, cut, width - cut, False, 1, 1),
-        (8, cut, width - cut, False, -1, -1),
-        (0, 0, cut, True, 1, 1),
-        (8, 0, cut, True, -1, -1),
+        (0, upper, width - upper, False, 1, 1),
+        (8, lower, width - lower, False, -1, -1),
+        (0, 0, upper, True, 1, 1),
+        (8, 0, lower, True, -1, -1),
     )
 
 
@@ -156,6 +156,8 @@
     y, core = group // 2, group % 2
     hub = core == 1
 
+    turn = 1 - 2 * core
+
     def at(dx, dz, dy=0, to_core=core):
         to = (x + dx + NX) % NX * NZ + (z + dz + NZ) % NZ
         return ((y + dy + NY) % NY * 2 + to_core, to)
@@ -265,7 +267,7 @@
     def view(place):
         v, ox, oz = place
         row, column, columns, *_ = pieces[v]
-        source = (x - ox + NX) % NX * NZ + (z - oz + NZ) % NZ
+        source = (x - turn * ox + NX) % NX * NZ + (z - oz + NZ) % NZ
         start = pl.multiple_of(source * 16 + row, 8)
         return rep.at[pl.ds(start, ROWS), pl.ds(column, columns)]
 
@@ -286,7 +288,7 @@
             copy_of(taken, slot[group[0]], at(1, 0)).wait_recv()
         for send in plan[step][1] if step < len(plan) else ():
             axis, way, there = send
-            peer = at(way, 0) if axis == "x" else at(0, way)
+            peer = at(turn * way, 0) if axis == "x" else at(0, way)
             copy_of(view(source_of(send)), slot[there], peer).start()
 
     correct_one = 1.0 - 0.9**10

time: 62.1 us -> 61.8 us (level)
  no operation moved by 1% of the time
where the time goes in v5:
time: 61.8 us; the launch traced here: 61.7 us
  Pallas kernels  61.1 us (99%)
  between operations  0.64 us (1%)
    pallas_call x1, Pallas kernels, on_device(): pl.pallas_call(functools.partial(step_kernel, entries), out_shape=(pltpu....  57.7 us
    pallas_call x1, Pallas kernels, on_device(): pl.pallas_call(store_kernel, out_shape=(jax.ShapeDtypeStruct((rows, width...  3.44 us

profile of v5, /device:TPU:8, one launch (start us, length us, event | category | flops | bytes accessed | tf_op | source)
XLA Modules:
  0.0 61.7 jit_solution(12102146688595414493)
XLA Ops:
  0.6 57.7 %step.1 = (bf16[512,7168]{1,0:T(8,128)(2,1)S(1)}, f32[16,7168]{1,0:T(8,128)S(1)}, f32[16,7168]{1,0:T(8,128)S(1)}, f32[16,7168]{1,0:T(8,128)S(1)}) custom-call(f32[16,7168]{1,0:T(8,128)} %p_hbm.1, bf16[16,7168]{1,0:T(8,128)(2,1)} %g_hbm.1, f32[16,7168]{1,0:T(8,128)} %m_hbm.1, f32[16,7168]{1,0:T(8,128)} %v_hbm.1), custom_call_target="tpu_custom_call" | custom-call | tf_op jit(solution)/shard_map/step/pallas_call | solution.py:356
  58.3 3.4 %store.1 = (f32[16,7168]{1,0:T(8,128)}, f32[16,7168]{1,0:T(8,128)}, f32[16,7168]{1,0:T(8,128)}, bf16[512,7168]{1,0:T(8,128)(2,1)}) custom-call(bf16[512,7168]{1,0:T(8,128)(2,1)S(1)} %get-tuple-element.8.rep, f32[16,7168]{1,0:T(8,128)S(1)} %get-tuple-element.9.p_new, f32[16,7168]{1,0:T(8,128)S(1)} %get-tuple-element.10.m_new, ...), custom_call_target="tpu_custom_call" | custom-call | tf_op jit(solution)/shard_map/store/pallas_call | solution.py:386
